TPU v7x, 32 devices: a whole 2x2x4 slice. The times are simulated.
32 devices in a mesh: inst: 4 (over x, core), shard: 8 (over z, y).
Axes of the slice: x: 2, y: 2, z: 4, core: 2. Of those that a mesh axis runs over, the one named last changes fastest.
Arguments:
- tokens: bfloat16 [2048, 5120], P(('inst', 'shard')), may hold values from -600 to 600
- norm_gain: float32 [5120], P(('inst', 'shard')), may hold values from 0.1 to 1.9
- master_qkv: float32 [5120, 7168], P(('inst', 'shard')), may hold values from -0.078125 to 0.078125
- qkv_bias: float32 [7168], P(('inst', 'shard')), may hold values from -3 to 3
Outputs:
- qkv_out: bfloat16 [32, 512, 896], P(('inst', 'shard'))
All inputs are finite; a program needn't handle non-finite values.
Results may differ from a plain program's by a relative error of at most 0.0062.
Values may be sent and summed in bfloat16 or wider, within the bound.
No kernel may reach another device: no remote copies, remote signals or barrier semaphores. Data moves between devices by JAX's collectives and lax.ppermute only.
A program may use at most 64 MiB of HBM per device.

v0:
```python
import jax
import jax.numpy as jnp
from jax import lax
from jax.sharding import PartitionSpec as P

QHEADS = 40
KVHEADS = 8
HEAD_DIM = 128
TP = 8


EPSILON = 1e-06


def partner_2(value, axis, distance):
    mask = 2**distance
    pairs = [(source, source ^ mask) for source in range(lax.axis_size(axis))]
    return lax.ppermute(value, axis, pairs)


def rank_columns(matrix):
    query_cols = QHEADS * HEAD_DIM
    pair_cols = KVHEADS * HEAD_DIM
    leading = matrix.shape[:-1]
    query = matrix[..., :query_cols].reshape(leading + (TP, query_cols // TP))
    keys = matrix[..., query_cols : query_cols + pair_cols].reshape(leading + (TP, pair_cols // TP))
    values = matrix[..., query_cols + pair_cols :].reshape(leading + (TP, pair_cols // TP))
    return jnp.concatenate([query, keys, values], axis=-1)


def normalize(tokens, gain):
    floats = tokens.astype(jnp.float32)
    scale = lax.rsqrt(jnp.mean(floats * floats, axis=-1, keepdims=True) + EPSILON)
    return (floats * scale * gain.astype(jnp.float32)).astype(jnp.bfloat16)


def per_device(tokens, norm_gain, master_qkv, qkv_bias):
    shard_count = lax.axis_size("shard")
    local_rows = master_qkv.shape[0]
    rank_width = master_qkv.shape[1] // TP
    gain_full, bias_full = (
        lax.all_gather(norm_gain.astype(jnp.bfloat16), ("inst", "shard"), axis=0, tiled=True),
        lax.all_gather(qkv_bias.astype(jnp.bfloat16), ("inst", "shard"), axis=0, tiled=True),
    )
    normed = normalize(tokens, gain_full)
    shard_pos = lax.axis_index("shard")
    rank_index = shard_pos % TP
    bit_count = TP.bit_length() - 1
    bit_order = list(range(bit_count))
    group_rows = normed
    for bit_pos in bit_order:
        partner = partner_2(group_rows, "shard", bit_pos)
        lower = jnp.bitwise_and(jnp.right_shift(shard_pos, bit_pos), 1) == 0
        group_rows = jnp.where(
            lower,
            jnp.concatenate([group_rows, partner], 0),
            jnp.concatenate([partner, group_rows], 0),
        )
    copies = shard_count // TP
    inst_block = shard_count * local_rows
    rows_low = master_qkv.astype(jnp.bfloat16)
    ranked = jnp.transpose(rank_columns(rows_low), (1, 0, 2))
    spread = jnp.broadcast_to(ranked[None], (copies,) + ranked.shape)
    outgoing = spread.reshape(shard_count, rows_low.shape[0], rank_width)
    arrived = lax.all_to_all(outgoing, "shard", split_axis=0, concat_axis=0, tiled=True).reshape(
        inst_block, rank_width
    )
    product = jnp.dot(
        group_rows,
        lax.all_gather(arrived, "inst", axis=0, tiled=True),
        preferred_element_type=jnp.float32,
    )
    bias_ranks = rank_columns(bias_full)
    bias_mine = lax.dynamic_index_in_dim(bias_ranks, rank_index, 0, keepdims=False)
    result = (product + bias_mine.astype(jnp.float32)).astype(jnp.bfloat16)
    return result[None]


def solution(mesh):
    in_specs = (
        P(("inst", "shard"), None),
        P(("inst", "shard")),
        P(("inst", "shard"), None),
        P(("inst", "shard")),
    )
    out_specs = P(("inst", "shard"), None, None)
    return jax.shard_map(
        per_device, mesh=mesh, in_specs=in_specs, out_specs=out_specs, check_vma=False
    )
```

profile of v0, /device:TPU:0, one launch (start us, length us, event | category | flops | bytes accessed | tf_op | source)
XLA Modules:
  0.0 292.7 jit_solution(10127492376784495317)
XLA Ops:
  6.5 0.0 all-gather.2.cloned.1.call-start
  6.5 2.6 convert_element_type.27
  9.2 0.1 slice.46
  9.3 0.3 copy.7
  9.6 0.1 copy.8
  9.6 0.1 copy.9
  9.7 0.2 maximum_bitcast_fusion
  9.9 0.3 copy.6
  10.2 0.0 copy-start.1
  10.2 0.0 copy-start.2
  10.2 0.0 copy-start
  10.3 59.9 %all_to_all.5 = bf16[8,160,896]{2,1,0:T(8,128)(2,1)} all-to-all(bf16[8,160,896]{2,1,0:T(8,128)(2,1)S(1)} %copy.6), channel_id=1, replica_groups=mesh['inst'=4,'shard'=8] {'shard'}, dimensions={0} | all-to-all | bytes 4587520 | tf_op jit(solution)/shard_map/all_to_all | solution.py:65
  70.1 0.0 all-gather.2.cloned.1.call-update
  70.1 0.0 copy-done.1
  70.2 0.0 copy-done.2
  70.2 0.2 dynamic-update-slice
  70.5 0.2 dynamic-update-slice.1
  70.7 40.0 %all-reduce.2 = (bf16[5120]{0:T(1024)(128)(2,1)S(1)}, bf16[7168]{0:T(1024)(128)(2,1)S(1)}) all-reduce(bf16[5120]{0:T(1024)(128)(2,1)S(1)} %dynamic-update-slice, bf16[7168]{0:T(1024)(128)(2,1)S(1)} %dynamic-update-slice.1), channel_id=1, replica_groups=mesh['inst'=4,'shard'=8] {'inst','shard'}, use_global_device_ids=true, to_apply=%add | all-reduce | flops 12288 | bytes 49152
  110.6 0.0 copy-done
  110.6 0.2 fusion.8
  110.9 0.2 fusion.10
  111.1 2.4 collective-permute-start
  113.5 14.4 %collective-permute-done = bf16[64,5120]{1,0:T(8,128)(2,1)S(1)} collective-permute-done((bf16[64,5120]{1,0:T(8,128)(2,1)S(1)}, bf16[64,5120]{1,0:T(8,128)(2,1)S(1)}, u32[]{:S(2)}, u32[]{:S(2)}) %collective-permute-start) | collective-permute-done | bytes 655392 | tf_op jit(solution)/shard_map/ppermute | solution.py:18
  127.9 0.3 maximum_select_fusion.7
  128.1 1.8 collective-permute-start.1
  129.9 27.9 %collective-permute-done.1 = bf16[128,5120]{1,0:T(8,128)(2,1)S(1)} collective-permute-done((bf16[128,5120]{1,0:T(8,128)(2,1)S(1)}, bf16[128,5120]{1,0:T(8,128)(2,1)S(1)}, u32[]{:S(2)}, u32[]{:S(2)}) %collective-permute-start.1) | collective-permute-done | bytes 1310752 | tf_op jit(solution)/shard_map/ppermute | solution.py:18
  157.9 2.0 maximum_select_fusion.2
  159.9 1.8 collective-permute-start.2
  161.8 112.3 %collective-permute-done.2 = bf16[256,5120]{1,0:T(8,128)(2,1)S(1)} collective-permute-done((bf16[256,5120]{1,0:T(8,128)(2,1)}, bf16[256,5120]{1,0:T(8,128)(2,1)S(1)}, u32[]{:S(2)}, u32[]{:S(2)}) %collective-permute-start.2) | collective-permute-done | bytes 2621472 | tf_op jit(solution)/shard_map/ppermute | solution.py:18
  274.1 0.0 all-gather.2.cloned.1.call-done
  274.1 11.8 %fusion.7 = bf16[1,512,896]{2,1,0:T(8,128)(2,1)} fusion(bf16[5120,896]{1,0:T(8,128)(2,1)} %all-gather.2.cloned.1.call-done, bf16[256,5120]{1,0:T(8,128)(2,1)S(1)} %collective-permute-done.2, bf16[256,5120]{1,0:T(8,128)(2,1)} %maximum_select_fusion.2, pred[]{:T(512)S(6)} %eq.11, f32[896]{0:T(1024)S(1)} %convert_reduce_fusion), kind=kOutput, calls=%fused_computation.13 | convolution fusion | flops 4722130944 | bytes 15339009 | tf_op jit(solution)/shard_map/dot_general | solution.py:68
  (11 shorter events, 0.1 us)
Async XLA Ops:
  6.5 267.6 %all-gather.2.cloned.1.call-start = ((), (), s32[]{:S(2)}) async-start(), calls=%async_computation.1 | async-start | bytes 11468800 | tf_op jit(solution)/shard_map/all_gather | solution.py:70
  10.2 59.9 %copy-start.1 = (f32[160]{0:T(256)S(1)}, f32[160]{0:T(256)}, u32[]{:S(2)}) copy-start(f32[160]{0:T(256)} %param.5) | copy-start | bytes 1924
  10.2 59.9 %copy-start.2 = (f32[224]{0:T(256)S(1)}, f32[224]{0:T(256)}, u32[]{:S(2)}) copy-start(f32[224]{0:T(256)} %param.7) | copy-start | bytes 2692
  10.2 100.4 %copy-start = (bf16[64,5120]{1,0:T(8,128)(2,1)S(1)}, bf16[64,5120]{1,0:T(8,128)(2,1)}, u32[]{:S(2)}) copy-start(bf16[64,5120]{1,0:T(8,128)(2,1)} %param.4) | copy-start | bytes 1966084
  111.1 16.7 %collective-permute-start = (bf16[64,5120]{1,0:T(8,128)(2,1)S(1)}, bf16[64,5120]{1,0:T(8,128)(2,1)S(1)}, u32[]{:S(2)}, u32[]{:S(2)}) collective-permute-start(bf16[64,5120]{1,0:T(8,128)(2,1)S(1)} %fusion.10), channel_id=1, source_target_pairs={{0,1},{1,0},{2,3},{3,2},{4,5},{5,4},{6,7},{7,6},{8,9},{9,8},{10,11... | collective-permute-start | bytes 1966088 | tf_op jit(solution)/shard_map/ppermute | solution.py:18
  128.1 29.8 %collective-permute-start.1 = (bf16[128,5120]{1,0:T(8,128)(2,1)S(1)}, bf16[128,5120]{1,0:T(8,128)(2,1)S(1)}, u32[]{:S(2)}, u32[]{:S(2)}) collective-permute-start(bf16[128,5120]{1,0:T(8,128)(2,1)S(1)} %maximum_select_fusion.7), channel_id=1, source_target_pairs={{0,2},{1,3},{2,0},{3,1},{4,6},{5,7},{6,4},{7,5},{8,10},{9,11},{10,... | collective-permute-start | bytes 3932168 | tf_op jit(solution)/shard_map/ppermute | solution.py:18
  159.9 114.2 %collective-permute-start.2 = (bf16[256,5120]{1,0:T(8,128)(2,1)}, bf16[256,5120]{1,0:T(8,128)(2,1)S(1)}, u32[]{:S(2)}, u32[]{:S(2)}) collective-permute-start(bf16[256,5120]{1,0:T(8,128)(2,1)} %maximum_select_fusion.2), channel_id=1, source_target_pairs={{0,4},{1,5},{2,6},{3,7},{4,0},{5,1},{6,2},{7,3},{8,12},{9,13},{10,... | collective-permute-start | bytes 7864328 | tf_op jit(solution)/shard_map/ppermute | solution.py:18
Sparse Core Ops, SparseCore 0:
  70.3 62.5 all-gather.1
where the time goes:
time: 293 us
  waiting for transfers between devices  155 us (53%)
  blocking collectives  99.8 us (34%)
  between operations  13.6 us (5%)
  matrix products  11.8 us (4%)
  starting transfers between devices  6 us (2%)
  other arithmetic  5.53 us (2%)
    ppermute x3, waiting for transfers between devices, partner_2(): return lax.ppermute(value, axis, pairs)  155 us
    all_to_all x1, blocking collectives, per_device(): lax.all_to_all(outgoing, 'shard', split_axis=0, concat_axis=0, tiled=True)  59.9 us
    unnamed x1, blocking collectives  40 us
    dot_general x1, matrix products, per_device(): jnp.dot(group_rows, lax.all_gather(arrived, 'inst', axis=0, tiled=True),...  11.8 us
    ppermute x3, starting transfers between devices, partner_2(): return lax.ppermute(value, axis, pairs)  6 us
  transfers between devices with their start and end apart: 4, of which 3 were waited for; matrix products, arithmetic and copies ran while one was open for 1% of the time, Pallas kernels for 0%

commit v1 on v0

v1 whole, which is shorter than its diff:
```python
import functools

import jax
import jax.numpy as jnp
from jax import lax
from jax.experimental import pallas as pl
from jax.experimental.pallas import tpu as pltpu
from jax.sharding import PartitionSpec as P

QHEADS = 40
KVHEADS = 8
HEAD_DIM = 128
TP = 8
QUERY_COLS = QHEADS * HEAD_DIM
PAIR_COLS = KVHEADS * HEAD_DIM

EPSILON = 1e-06

QUAD = TP // 2
LOW = 4
VMEM = pl.BlockSpec(memory_space=pltpu.VMEM)
ANY = pl.BlockSpec(memory_space=pl.ANY)


def exchange(value, axis, mask):
    pairs = [(source, source ^ mask) for source in range(lax.axis_size(axis))]
    return lax.ppermute(value, axis, pairs)


def bit_of(index, position):
    return jnp.bitwise_and(jnp.right_shift(index, position), 1)


def ordered(mine, theirs, upper):
    return jnp.where(
        upper == 0, jnp.concatenate([mine, theirs], 0), jnp.concatenate([theirs, mine], 0)
    )


def bits_of(count):
    return range(count.bit_length() - 1)


def place():
    rank = lax.rem(lax.axis_index("shard"), TP)
    return lax.div(rank, QUAD), lax.rem(rank, QUAD)


def bf16_shapes(shapes):
    return [jax.ShapeDtypeStruct(shape, jnp.bfloat16) for shape in shapes]


def token_body(tokens_ref, keep_ref, give_ref):
    half, _ = place()
    low = lax.rem(lax.axis_index("inst"), LOW)
    width = tokens_ref.shape[1] // (2 * LOW)
    floats = tokens_ref[...].astype(jnp.float32)
    scale = lax.rsqrt(jnp.mean(floats * floats, axis=-1, keepdims=True) + EPSILON)
    for out_ref, part in ((keep_ref, half), (give_ref, 1 - half)):
        for mask in range(LOW):
            start = (jnp.bitwise_xor(low, mask) * 2 + part) * width
            block = tokens_ref[:, pl.ds(pl.multiple_of(start, 128), width)].astype(jnp.float32)
            out_ref[:, mask * width : (mask + 1) * width] = (block * scale).astype(jnp.bfloat16)


def prepare_tokens(tokens):
    count, features = tokens.shape
    return pl.pallas_call(
        token_body,
        out_shape=bf16_shapes([(count, features // 2)] * 2),
        in_specs=[VMEM],
        out_specs=[VMEM] * 2,
    )(tokens)


def weight_body(other, cuts, gain_ref, master_ref, *refs):
    out_refs, (scratch, sems) = refs[:-2], refs[-2:]
    half, quad_pos = place()
    part = 1 - half if other else half
    spans = ((0, QUERY_COLS // TP), (QUERY_COLS, PAIR_COLS // TP), (QUERY_COLS + PAIR_COLS, PAIR_COLS // TP))
    copies = []
    for mask in range(QUAD):
        rank = part * QUAD + jnp.bitwise_xor(quad_pos, mask)
        offset = 0
        for number, (first, width) in enumerate(spans):
            start = pl.multiple_of(first + rank * width, 128)
            copies.append(
                pltpu.make_async_copy(
                    master_ref.at[:, pl.ds(start, width)],
                    scratch.at[mask, :, pl.ds(offset, width)],
                    sems.at[mask, number],
                )
            )
            offset += width
    for copy in copies:
        copy.start()
    gain = gain_ref[...].astype(jnp.bfloat16).astype(jnp.float32)
    for mask in range(QUAD):
        for number in range(len(spans)):
            copies[mask * len(spans) + number].wait()
        for chunk, (start, stop) in enumerate(cuts):
            block = scratch[mask, :, start:stop].astype(jnp.bfloat16).astype(jnp.float32)
            out_refs[chunk * QUAD + mask][...] = (block * gain).astype(jnp.bfloat16)


def prepare_weights(gain, master, other, cuts):
    rows, width = master.shape
    outs = pl.pallas_call(
        functools.partial(weight_body, other, cuts),
        out_shape=bf16_shapes([(rows, stop - start) for start, stop in cuts for _ in range(QUAD)]),
        in_specs=[VMEM, ANY],
        out_specs=[VMEM] * (QUAD * len(cuts)),
        scratch_shapes=[
            pltpu.VMEM((QUAD, rows, width // TP), jnp.float32),
            pltpu.SemaphoreType.DMA((QUAD, 3)),
        ],
    )(gain, master)
    return [outs[chunk * QUAD : (chunk + 1) * QUAD] for chunk in range(len(cuts))]


def assemble_body(*refs):
    out_ref = refs[-1]
    _, quad_pos = place()
    rows = refs[0].shape[0]
    for mask in range(QUAD):
        start = pl.multiple_of(jnp.bitwise_xor(quad_pos, mask) * rows, 16)
        out_ref[pl.ds(start, rows), :] = refs[mask][...]


def assemble(pieces):
    rows, width = pieces[0].shape
    if rows % 16 == 0:
        return pl.pallas_call(
            assemble_body,
            out_shape=bf16_shapes([(QUAD * rows, width)])[0],
            in_specs=[VMEM] * QUAD,
            out_specs=VMEM,
        )(*pieces)
    _, quad_pos = place()
    step = 1
    while step < QUAD:
        swap = jnp.bitwise_and(quad_pos, step) != 0
        pieces = [jnp.where(swap, pieces[at ^ step], pieces[at]) for at in range(QUAD)]
        step *= 2
    return jnp.concatenate(pieces, 0)


def spread_rows(pieces):
    shard_pos, instance = lax.axis_index("shard"), lax.axis_index("inst")
    block = assemble(
        [pieces[0]] + [exchange(pieces[mask], "shard", mask) for mask in range(1, QUAD)]
    )
    for position in bits_of(lax.axis_size("shard") // TP):
        theirs = exchange(block, "shard", TP << position)
        block = ordered(block, theirs, bit_of(shard_pos, position + TP.bit_length() - 1))
    for position in bits_of(lax.axis_size("inst") // LOW):
        theirs = exchange(block, "inst", LOW << position)
        block = ordered(block, theirs, bit_of(instance, position + LOW.bit_length() - 1))
    across = exchange(block, "inst", 2)
    return [block, exchange(block, "inst", 1), across, exchange(across, "inst", 1)]


def matmul_body(*refs):
    token_refs, weight_refs = refs[:TP], refs[TP : TP + LOW]
    out_ref, rows_ref = refs[TP + LOW :]
    count = token_refs[0].shape[0]

    @pl.when(pl.program_id(0) == 0)
    def _():
        for number, token_ref in enumerate(token_refs):
            rows_ref[number * count : (number + 1) * count, :] = token_ref[...]

    depth = weight_refs[0].shape[0]
    total = None
    for number, weight_ref in enumerate(weight_refs):
        term = jnp.dot(
            rows_ref[:, number * depth : (number + 1) * depth],
            weight_ref[...],
            preferred_element_type=jnp.float32,
        )
        total = term if total is None else total + term
    out_ref[...] = total.astype(out_ref.dtype)


def matmul(token_pieces, blocks, dtype):
    count, features = token_pieces[0].shape
    depth, width = blocks[0].shape
    tile = 256 if width % 256 == 0 else 128
    rows = TP * count
    return pl.pallas_call(
        matmul_body,
        grid=(width // tile,),
        out_shape=jax.ShapeDtypeStruct((rows, width), dtype),
        in_specs=[pl.BlockSpec((count, features), lambda step: (0, 0))] * TP
        + [pl.BlockSpec((depth, tile), lambda step: (0, step))] * LOW,
        out_specs=pl.BlockSpec((rows, tile), lambda step: (0, step)),
        scratch_shapes=[pltpu.VMEM((rows, features), jnp.bfloat16)],
        cost_estimate=pl.CostEstimate(
            flops=2 * rows * features * width,
            bytes_accessed=2 * (rows * features + features * width + rows * width),
            transcendentals=0,
        ),
    )(*token_pieces, *blocks)


def finish_body(*refs):
    mine_ref, bias_ref, out_ref = refs[0], refs[1], refs[-1]
    half, quad_pos = place()
    rank = half * QUAD + quad_pos
    count = mine_ref.shape[0] // TP
    spans = ((0, QUERY_COLS // TP), (QUERY_COLS, PAIR_COLS // TP), (QUERY_COLS + PAIR_COLS, PAIR_COLS // TP))
    bias = jnp.concatenate(
        [
            bias_ref[:, pl.ds(pl.multiple_of(first + rank * width, 128), width)]
            for first, width in spans
        ],
        axis=1,
    ).astype(jnp.float32)
    for number in range(TP):
        rows = slice(number * count, (number + 1) * count)
        crossed = slice((number ^ QUAD) * count, ((number ^ QUAD) + 1) * count)
        place_out = pl.multiple_of(jnp.bitwise_xor(rank, number) * count, count)
        start = 0
        for part_ref in refs[2:-1]:
            stop = start + part_ref.shape[1]
            value = mine_ref[rows, start:stop] + part_ref[crossed, :].astype(jnp.float32)
            out_ref[0, pl.ds(place_out, count), start:stop] = (
                value + bias[:, start:stop]
            ).astype(jnp.bfloat16)
            start = stop


def finish(mine, bias, parts):
    return pl.pallas_call(
        finish_body,
        out_shape=jax.ShapeDtypeStruct((1,) + mine.shape, jnp.bfloat16),
        in_specs=[VMEM] * (2 + len(parts)),
        out_specs=VMEM,
    )(mine, bias, *parts)


def gather_bias(bias):
    rows = bias.astype(jnp.bfloat16).astype(jnp.float32).reshape(1, -1)
    shards, instances = lax.axis_size("shard"), lax.axis_size("inst")
    index = lax.axis_index("inst") * shards + lax.axis_index("shard")
    for position in bits_of(shards):
        rows = jnp.concatenate([rows, exchange(rows, "shard", 1 << position)], 0)
    for position in bits_of(instances):
        rows = jnp.concatenate([rows, exchange(rows, "inst", 1 << position)], 0)
    order = jnp.bitwise_xor(jnp.arange(shards * instances), index)
    return rows[order].reshape(1, -1)


def gather_quad(piece):
    along = exchange(piece, "shard", 2)
    return [piece, exchange(piece, "shard", 1), along, exchange(along, "shard", 1)]


def per_device(tokens, norm_gain, master_qkv, qkv_bias):
    instances = lax.axis_size("inst")
    copies = lax.axis_size("shard") // TP
    local_rows = master_qkv.shape[0]
    rank_width = master_qkv.shape[1] // TP
    count, features = tokens.shape

    if instances * copies > LOW:
        tokens = tokens.reshape(count, instances // LOW, LOW, copies, 2, QUAD * local_rows)
        tokens = jnp.transpose(tokens, (0, 2, 4, 1, 3, 5)).reshape(count, features)
    keep, give = prepare_tokens(tokens)
    got = exchange(give, "shard", QUAD)
    group = gather_quad(keep) + gather_quad(got)

    cut = (rank_width // 2 + HEAD_DIM - 1) // HEAD_DIM * HEAD_DIM
    gain = norm_gain[:, None]
    theirs = prepare_weights(gain, master_qkv, True, ((0, cut), (cut, rank_width)))
    mine = prepare_weights(gain, master_qkv, False, ((0, rank_width),))

    parts = []
    for pieces in theirs:
        partial = matmul(group, spread_rows(pieces), jnp.bfloat16)
        parts.append(exchange(partial, "shard", QUAD))
    own = matmul(group, spread_rows(mine[0]), jnp.float32)
    return finish(own, gather_bias(qkv_bias), parts)


def solution(mesh):
    in_specs = (
        P(("inst", "shard"), None),
        P(("inst", "shard")),
        P(("inst", "shard"), None),
        P(("inst", "shard")),
    )
    out_specs = P(("inst", "shard"), None, None)
    return jax.shard_map(
        per_device, mesh=mesh, in_specs=in_specs, out_specs=out_specs, check_vma=False
    )
```

time: 293 us -> 145 us (0.49)
  blocking collectives: 99.8 us -> 0 us
  waiting for transfers between devices: 155 us -> 65.8 us
  Pallas kernels: 0 us -> 39.8 us
  starting transfers between devices: 6 us -> 32.7 us
  between operations: 13.6 us -> 0.2 us
  matrix products: 11.8 us -> 0 us
  other arithmetic: 5.53 us -> 0.04 us
  local copies, waits for them, and re-layouts: 1.37 us -> 6.04 us
    ppermute x3 -> x32, waiting for transfers between devices: 155 us -> 65.8 us  [exchange(): return lax.ppermute(value, axis, pairs)]
    all_to_all x1 -> x0, blocking collectives: 59.9 us -> none  [per_device(): lax.all_to_all(outgoing, 'shard', split_axis=0, concat_axis=0, tiled=True)]
    unnamed x1 -> x0, blocking collectives: 40 us -> none
    pallas_call x0 -> x10, Pallas kernels: none -> 39.8 us  [the longest x3 21.1 us: matmul(): pl.pallas_call(matmul_body, grid=(width // tile,), out_shape=jax.ShapeDty...]
    ppermute x3 -> x32, starting transfers between devices: 6 us -> 32.7 us  [exchange(): return lax.ppermute(value, axis, pairs)]
    dot_general x1 -> x0, matrix products: 11.8 us -> none  [per_device(): jnp.dot(group_rows, lax.all_gather(arrived, 'inst', axis=0, tiled=True),...]
  transfers between devices with their start and end apart: 4 -> 32, of which waited for: 3 -> 11; matrix products, arithmetic and copies ran while one was open for 1% -> 1% of each run, Pallas kernels for 0% -> 23%
where the time goes in v1:
time: 145 us
  waiting for transfers between devices  65.8 us (45%)
  Pallas kernels  39.8 us (27%)
  starting transfers between devices  32.7 us (23%)
  local copies, waits for them, and re-layouts  6.04 us (4%)
    ppermute x32, waiting for transfers between devices, exchange(): return lax.ppermute(value, axis, pairs)  65.8 us
    ppermute x32, starting transfers between devices, exchange(): return lax.ppermute(value, axis, pairs)  32.7 us
    pallas_call x3, Pallas kernels, matmul(): pl.pallas_call(matmul_body, grid=(width // tile,), out_shape=jax.ShapeDty...  21.1 us
    pallas_call x2, Pallas kernels, prepare_weights(): pl.pallas_call(functools.partial(weight_body, other, cuts), out_shape=bf1...  7.19 us
    pallas_call x3, Pallas kernels, assemble(): pl.pallas_call(assemble_body, out_shape=bf16_shapes([(QUAD * rows, width)...  6.44 us
    unnamed x44, local copies, waits for them, and re-layouts  3.26 us
  transfers between devices with their start and end apart: 32, of which 11 were waited for; matrix products, arithmetic and copies ran while one was open for 1% of the time, Pallas kernels for 23%

profile of v1, /device:TPU:0, one launch (start us, length us, event | category | flops | bytes accessed | tf_op | source)
XLA Modules:
  0.0 144.6 jit_solution(5021927160694772879)
XLA Ops:
  0.0 1.4 copy.5.gain_ref
  1.4 3.6 %shard_map.47 = (bf16[160,896]{1,0:T(8,128)(2,1)}, bf16[160,896]{1,0:T(8,128)(2,1)}, bf16[160,896]{1,0:T(8,128)(2,1)}, bf16[160,896]{1,0:T(8,128)(2,1)}) custom-call(f32[160,1]{1,0:T(8,128)} %copy.5.gain_ref, f32[160,7168]{1,0:T(8,128)} %master_ref.3), custom_call_target="tpu_custom_call" | custom-call | tf_op jit(solution)/shard_map/pallas_call | solution.py:108
  5.0 3.1 %collective-permute-start.7 = (bf16[160,896]{1,0:T(8,128)(2,1)}, bf16[160,896]{1,0:T(8,128)(2,1)S(1)}, u32[]{:S(2)}, u32[]{:S(2)}) collective-permute-start(bf16[160,896]{1,0:T(8,128)(2,1)} %get-tuple-element.22), channel_id=1, source_target_pairs={{0,1},{1,0},{2,3},{3,2},{4,5},{5,4},{6,7},{7,6},{8,9},{9,8},{10,11... | collective-permute-start | bytes 860168 | tf_op jit(solution)/shard_map/ppermute | solution.py:27
  8.1 1.6 %collective-permute-start.8 = (bf16[160,896]{1,0:T(8,128)(2,1)}, bf16[160,896]{1,0:T(8,128)(2,1)S(1)}, u32[]{:S(2)}, u32[]{:S(2)}) collective-permute-start(bf16[160,896]{1,0:T(8,128)(2,1)} %get-tuple-element.23), channel_id=1, source_target_pairs={{0,2},{1,3},{2,0},{3,1},{4,6},{5,7},{6,4},{7,5},{8,10},{9,11},{10,... | collective-permute-start | bytes 860168 | tf_op jit(solution)/shard_map/ppermute | solution.py:27
  9.7 1.9 %collective-permute-start.13 = (f32[1,224]{1,0:T(1,128)S(1)}, f32[1,224]{1,0:T(1,128)S(1)}, u32[]{:S(2)}, u32[]{:S(2)}) collective-permute-start(f32[1,224]{1,0:T(1,128)S(1)} %bitcast.4), channel_id=1, source_target_pairs={{0,1},{1,0},{2,3},{3,2},{4,5},{5,4},{6,7},{7,6},{8,9},{9,8},{10,11... | collective-permute-start | bytes 2696 | tf_op jit(solution)/shard_map/ppermute | solution.py:27
  11.6 3.6 %collective-permute-done.7.refs_1_ = bf16[160,896]{1,0:T(8,128)(2,1)S(1)} collective-permute-done((bf16[160,896]{1,0:T(8,128)(2,1)}, bf16[160,896]{1,0:T(8,128)(2,1)S(1)}, u32[]{:S(2)}, u32[]{:S(2)}) %collective-permute-start.7) | collective-permute-done | bytes 286752 | tf_op jit(solution)/shard_map/ppermute | solution.py:27
  15.2 2.9 %collective-permute-done.8.refs_2_ = bf16[160,896]{1,0:T(8,128)(2,1)S(1)} collective-permute-done((bf16[160,896]{1,0:T(8,128)(2,1)}, bf16[160,896]{1,0:T(8,128)(2,1)S(1)}, u32[]{:S(2)}, u32[]{:S(2)}) %collective-permute-start.8) | collective-permute-done | bytes 286752 | tf_op jit(solution)/shard_map/ppermute | solution.py:27
  18.0 4.5 %collective-permute-done.9.refs_3_ = bf16[160,896]{1,0:T(8,128)(2,1)S(1)} collective-permute-done((bf16[160,896]{1,0:T(8,128)(2,1)}, bf16[160,896]{1,0:T(8,128)(2,1)S(1)}, u32[]{:S(2)}, u32[]{:S(2)}) %collective-permute-start.9) | collective-permute-done | bytes 286752 | tf_op jit(solution)/shard_map/ppermute | solution.py:27
  22.5 0.7 copy-done.14
  23.3 2.4 %shard_map.48.refs_8_ = bf16[640,896]{1,0:T(8,128)(2,1)} custom-call(bf16[160,896]{1,0:T(8,128)(2,1)} %get-tuple-element.21.refs_0_, bf16[160,896]{1,0:T(8,128)(2,1)} %copy-done.12, bf16[160,896]{1,0:T(8,128)(2,1)} %copy-done.13, bf16[160,896]{1,0:T(8,128)(2,1)} %copy-done.14), custom_call_target="tpu_custom_call" | custom-call | tf_op jit(solution)/shard_map/pallas_call | solution.py:133
  25.6 1.6 %collective-permute-start.11 = (bf16[640,896]{1,0:T(8,128)(2,1)}, bf16[640,896]{1,0:T(8,128)(2,1)}, u32[]{:S(2)}, u32[]{:S(2)}) collective-permute-start(bf16[640,896]{1,0:T(8,128)(2,1)} %shard_map.48.refs_8_), channel_id=1, source_target_pairs={{0,16},{8,24},{16,0},{24,8},{1,17},{9,25},{17,1},{25,9},{2,18},{10... | collective-permute-start | bytes 3440648 | tf_op jit(solution)/shard_map/ppermute | solution.py:27
  27.3 1.6 %collective-permute-start.14 = (f32[2,224]{1,0:T(2,128)S(1)}, f32[2,224]{1,0:T(2,128)S(1)}, u32[]{:S(2)}, u32[]{:S(2)}) collective-permute-start(f32[2,224]{1,0:T(2,128)S(1)} %pad_maximum_fusion.2), channel_id=1, source_target_pairs={{0,2},{1,3},{2,0},{3,1},{4,6},{5,7},{6,4},{7,5},{8,10},{9,11},{10,... | collective-permute-start | bytes 5384 | tf_op jit(solution)/shard_map/ppermute | solution.py:27
  28.9 3.6 %shard_map.50 = (bf16[160,512]{1,0:T(8,128)(2,1)}, bf16[160,512]{1,0:T(8,128)(2,1)}, bf16[160,512]{1,0:T(8,128)(2,1)}, bf16[160,512]{1,0:T(8,128)(2,1)}, bf16[16...) custom-call(f32[160,1]{1,0:T(8,128)} %copy.5.gain_ref, ...), custom_call_target="tpu_custom_call" | custom-call | tf_op jit(solution)/shard_map/pallas_call | solution.py:108
  32.5 1.6 %collective-permute-start.25 = (bf16[160,384]{1,0:T(8,128)(2,1)}, bf16[160,384]{1,0:T(8,128)(2,1)S(1)}, u32[]{:S(2)}, u32[]{:S(2)}) collective-permute-start(bf16[160,384]{1,0:T(8,128)(2,1)} %get-tuple-element.30), channel_id=1, source_target_pairs={{0,1},{1,0},{2,3},{3,2},{4,5},{5,4},{6,7},{7,6},{8,9},{9,8},{10,11... | collective-permute-start | bytes 368648 | tf_op jit(solution)/shard_map/ppermute | solution.py:27
  34.1 0.4 collective-permute-start.26
  34.6 1.5 %collective-permute-start.27 = (bf16[160,384]{1,0:T(8,128)(2,1)}, bf16[160,384]{1,0:T(8,128)(2,1)S(1)}, u32[]{:S(2)}, u32[]{:S(2)}) collective-permute-start(bf16[160,384]{1,0:T(8,128)(2,1)} %get-tuple-element.32), channel_id=1, source_target_pairs={{0,3},{1,2},{2,1},{3,0},{4,7},{5,6},{6,5},{7,4},{8,11},{9,10},{10,... | collective-permute-start | bytes 368648 | tf_op jit(solution)/shard_map/ppermute | solution.py:27
  36.1 0.0 collective-permute-done.14
  36.1 2.7 %collective-permute-start.15 = (f32[4,224]{1,0:T(4,128)S(1)}, f32[4,224]{1,0:T(4,128)S(1)}, u32[]{:S(2)}, u32[]{:S(2)}) collective-permute-start(f32[4,224]{1,0:T(4,128)S(1)} %pad_maximum_fusion.1), channel_id=1, source_target_pairs={{0,4},{1,5},{2,6},{3,7},{4,0},{5,1},{6,2},{7,3},{8,12},{9,13},{10,... | collective-permute-start | bytes 10760 | tf_op jit(solution)/shard_map/ppermute | solution.py:27
  38.8 1.9 %collective-permute-done.15 = f32[4,224]{1,0:T(4,128)S(1)} collective-permute-done((f32[4,224]{1,0:T(4,128)S(1)}, f32[4,224]{1,0:T(4,128)S(1)}, u32[]{:S(2)}, u32[]{:S(2)}) %collective-permute-start.15) | collective-permute-done | bytes 3616 | tf_op jit(solution)/shard_map/ppermute | solution.py:27
  40.7 1.5 %collective-permute-start.18 = (bf16[160,512]{1,0:T(8,128)(2,1)}, bf16[160,512]{1,0:T(8,128)(2,1)S(1)}, u32[]{:S(2)}, u32[]{:S(2)}) collective-permute-start(bf16[160,512]{1,0:T(8,128)(2,1)} %get-tuple-element.26), channel_id=1, source_target_pairs={{0,1},{1,0},{2,3},{3,2},{4,5},{5,4},{6,7},{7,6},{8,9},{9,8},{10,11... | collective-permute-start | bytes 491528 | tf_op jit(solution)/shard_map/ppermute | solution.py:27
  42.2 2.2 %shard_map.46 = (bf16[64,2560]{1,0:T(8,128)(2,1)}, bf16[64,2560]{1,0:T(8,128)(2,1)}) custom-call(bf16[64,5120]{1,0:T(8,128)(2,1)} %tokens_ref.1), custom_call_target="tpu_custom_call" | custom-call | tf_op jit(solution)/shard_map/pallas_call | solution.py:68
  44.4 1.6 %collective-permute-start.19 = (bf16[160,512]{1,0:T(8,128)(2,1)}, bf16[160,512]{1,0:T(8,128)(2,1)S(1)}, u32[]{:S(2)}, u32[]{:S(2)}) collective-permute-start(bf16[160,512]{1,0:T(8,128)(2,1)} %get-tuple-element.27), channel_id=1, source_target_pairs={{0,2},{1,3},{2,0},{3,1},{4,6},{5,7},{6,4},{7,5},{8,10},{9,11},{10,... | collective-permute-start | bytes 491528 | tf_op jit(solution)/shard_map/ppermute | solution.py:27
  45.9 0.0 collective-permute-done.26.refs_2_
  46.0 0.5 collective-permute-start.1
  46.4 1.1 collective-permute-start
  47.5 0.0 collective-permute-done.18.refs_1_
  47.5 2.4 %collective-permute-start.20 = (bf16[160,512]{1,0:T(8,128)(2,1)}, bf16[160,512]{1,0:T(8,128)(2,1)S(1)}, u32[]{:S(2)}, u32[]{:S(2)}) collective-permute-start(bf16[160,512]{1,0:T(8,128)(2,1)} %get-tuple-element.28), channel_id=1, source_target_pairs={{0,3},{1,2},{2,1},{3,0},{4,7},{5,6},{6,5},{7,4},{8,11},{9,10},{10,... | collective-permute-start | bytes 491528 | tf_op jit(solution)/shard_map/ppermute | solution.py:27
  49.9 2.0 %shard_map.53.refs_8_ = bf16[640,384]{1,0:T(8,128)(2,1)} custom-call(bf16[160,384]{1,0:T(8,128)(2,1)} %get-tuple-element.29.refs_0_, bf16[160,384]{1,0:T(8,128)(2,1)} %copy-done.18, bf16[160,384]{1,0:T(8,128)(2,1)} %copy-done.19, bf16[160,384]{1,0:T(8,128)(2,1)} %copy-done.20), custom_call_target="tpu_custom_call" | custom-call | tf_op jit(solution)/shard_map/pallas_call | solution.py:133
  51.9 0.5 collective-permute-start.29
  52.5 8.0 %collective-permute-done.20.refs_3_ = bf16[160,512]{1,0:T(8,128)(2,1)S(1)} collective-permute-done((bf16[160,512]{1,0:T(8,128)(2,1)}, bf16[160,512]{1,0:T(8,128)(2,1)S(1)}, u32[]{:S(2)}, u32[]{:S(2)}) %collective-permute-start.20) | collective-permute-done | bytes 163872 | tf_op jit(solution)/shard_map/ppermute | solution.py:27
  60.5 0.0 collective-permute-start.3
  60.5 0.0 collective-permute-done.1.refs_2_
  60.5 1.4 collective-permute-start.2
  62.0 2.0 %shard_map.51.refs_8_ = bf16[640,512]{1,0:T(8,128)(2,1)} custom-call(bf16[160,512]{1,0:T(8,128)(2,1)} %get-tuple-element.25.refs_0_, bf16[160,512]{1,0:T(8,128)(2,1)} %copy-done.15, bf16[160,512]{1,0:T(8,128)(2,1)} %copy-done.16, bf16[160,512]{1,0:T(8,128)(2,1)} %copy-done.17), custom_call_target="tpu_custom_call" | custom-call | tf_op jit(solution)/shard_map/pallas_call | solution.py:133
  64.0 0.0 collective-permute-done.refs_1_
  64.0 0.5 collective-permute-start.22
  64.6 7.7 %collective-permute-done.3.refs_4_ = bf16[64,2560]{1,0:T(8,128)(2,1)S(1)} collective-permute-done((bf16[64,2560]{1,0:T(8,128)(2,1)}, bf16[64,2560]{1,0:T(8,128)(2,1)S(1)}, u32[]{:S(2)}, u32[]{:S(2)}) %collective-permute-start.3) | collective-permute-done | bytes 327712 | tf_op jit(solution)/shard_map/ppermute | solution.py:27
  72.2 0.1 collective-permute-start.21
  72.3 0.8 copy-done.10
  73.1 0.0 collective-permute-start.5
  73.1 6.2 %collective-permute-done.4.refs_5_ = bf16[64,2560]{1,0:T(8,128)(2,1)S(1)} collective-permute-done((bf16[64,2560]{1,0:T(8,128)(2,1)S(1)}, bf16[64,2560]{1,0:T(8,128)(2,1)S(1)}, u32[]{:S(2)}, u32[]{:S(2)}) %collective-permute-start.4) | collective-permute-done | bytes 327712 | tf_op jit(solution)/shard_map/ppermute | solution.py:27
  79.3 0.0 collective-permute-done.11.refs_10_
  79.3 0.5 collective-permute-start.12
  79.8 2.7 %collective-permute-done.5.refs_6_ = bf16[64,2560]{1,0:T(8,128)(2,1)S(1)} collective-permute-done((bf16[64,2560]{1,0:T(8,128)(2,1)S(1)}, bf16[64,2560]{1,0:T(8,128)(2,1)S(1)}, u32[]{:S(2)}, u32[]{:S(2)}) %collective-permute-start.5) | collective-permute-done | bytes 327712 | tf_op jit(solution)/shard_map/ppermute | solution.py:27
  82.5 1.9 %collective-permute-start.6 = (bf16[64,2560]{1,0:T(8,128)(2,1)S(1)}, bf16[64,2560]{1,0:T(8,128)(2,1)S(1)}, u32[]{:S(2)}, u32[]{:S(2)}) collective-permute-start(bf16[64,2560]{1,0:T(8,128)(2,1)S(1)} %collective-permute-done.5.refs_6_), channel_id=1, source_target_pairs={{0,1},{1,0},{2,3},{3,2},{4,5},{5,4},{6,7},{7,6},{8,9},{9,8},{10,11... | collective-permute-start | bytes 983048 | tf_op jit(solution)/shard_map/ppermute | solution.py:27
  84.5 0.5 collective-permute-start.28
  85.0 6.2 %collective-permute-done.6.refs_7_ = bf16[64,2560]{1,0:T(8,128)(2,1)S(1)} collective-permute-done((bf16[64,2560]{1,0:T(8,128)(2,1)S(1)}, bf16[64,2560]{1,0:T(8,128)(2,1)S(1)}, u32[]{:S(2)}, u32[]{:S(2)}) %collective-permute-start.6) | collective-permute-done | bytes 327712 | tf_op jit(solution)/shard_map/ppermute | solution.py:27
  91.2 0.0 collective-permute-start.30
  91.3 0.6 collective-permute-start.16
  91.9 0.1 copy-done.7
  92.0 5.1 %shard_map.52 = bf16[512,512]{1,0:T(8,128)(2,1)} custom-call(bf16[64,2560]{1,0:T(8,128)(2,1)} %get-tuple-element.19.refs_0_, bf16[64,2560]{1,0:T(8,128)(2,1)} %copy-done.2, bf16[64,2560]{1,0:T(8,128)(2,1)} %copy-done.1, bf16[64,2560]{1,0:T(8,128)(2,1)} %copy-done.4, bf16[64,2560]{1,0:T(8,128)(2,1)} %copy-done.3, bf16[64,2560]{1,0:T(8,128)(2,1)} %copy-done.5, ...), custom_call_target="tpu_custom_call" | custom-call | flops 1342177280 | bytes 5767168 | tf_op jit(solution)/shard_map/pallas_call | solution.py:190
  97.0 0.0 collective-permute-done.28.refs_9_
  97.1 0.1 collective-permute-start.24
  97.1 5.8 %shard_map.54 = bf16[512,384]{1,0:T(8,128)(2,1)} custom-call(bf16[64,2560]{1,0:T(8,128)(2,1)} %get-tuple-element.19.refs_0_, bf16[64,2560]{1,0:T(8,128)(2,1)} %copy-done.2, bf16[64,2560]{1,0:T(8,128)(2,1)} %copy-done.1, bf16[64,2560]{1,0:T(8,128)(2,1)} %copy-done.4, bf16[64,2560]{1,0:T(8,128)(2,1)} %copy-done.3, bf16[64,2560]{1,0:T(8,128)(2,1)} %copy-done.5, ...), custom_call_target="tpu_custom_call" | custom-call | flops 1006632960 | bytes 4980736 | tf_op jit(solution)/shard_map/pallas_call | solution.py:190
  103.0 2.9 %collective-permute-start.31 = (bf16[512,384]{1,0:T(8,128)(2,1)}, bf16[512,384]{1,0:T(8,128)(2,1)S(1)}, u32[]{:S(2)}, u32[]{:S(2)}) collective-permute-start(bf16[512,384]{1,0:T(8,128)(2,1)} %shard_map.54), channel_id=1, source_target_pairs={{0,4},{1,5},{2,6},{3,7},{4,0},{5,1},{6,2},{7,3},{8,12},{9,13},{10,... | collective-permute-start | bytes 1179656 | tf_op jit(solution)/shard_map/ppermute | solution.py:27
  105.9 0.6 collective-permute-start.17
  106.5 3.2 %collective-permute-done.17 = f32[16,224]{1,0:T(8,128)S(1)} collective-permute-done((f32[16,224]{1,0:T(8,128)S(1)}, f32[16,224]{1,0:T(8,128)S(1)}, u32[]{:S(2)}, u32[]{:S(2)}) %collective-permute-start.17) | collective-permute-done | bytes 14368 | tf_op jit(solution)/shard_map/ppermute | solution.py:27
  109.7 0.6 gather_fusion
  110.3 0.7 reshape.27.refs_1_
  111.0 10.2 %shard_map.49.refs_0_ = f32[512,896]{1,0:T(8,128)} custom-call(bf16[64,2560]{1,0:T(8,128)(2,1)} %get-tuple-element.19.refs_0_, bf16[64,2560]{1,0:T(8,128)(2,1)} %copy-done.2, bf16[64,2560]{1,0:T(8,128)(2,1)} %copy-done.1, bf16[64,2560]{1,0:T(8,128)(2,1)} %copy-done.4, bf16[64,2560]{1,0:T(8,128)(2,1)} %copy-done.3, bf16[64,2560]{1,0:T(8,128)(2,1)} %copy-done.5, ...), custom_call_target="tpu_custom_call" | custom-call | flops 2348810240 | bytes 8126464 | tf_op jit(solution)/shard_map/pallas_call | solution.py:190
  121.3 18.9 %collective-permute-done.31.refs_3_ = bf16[512,384]{1,0:T(8,128)(2,1)S(1)} collective-permute-done((bf16[512,384]{1,0:T(8,128)(2,1)}, bf16[512,384]{1,0:T(8,128)(2,1)S(1)}, u32[]{:S(2)}, u32[]{:S(2)}) %collective-permute-start.31) | collective-permute-done | bytes 393248 | tf_op jit(solution)/shard_map/ppermute | solution.py:27
  140.1 0.8 copy-done.11
  140.9 0.8 copy-done.9
  141.7 2.9 %shard_map.55 = bf16[1,512,896]{2,1,0:T(8,128)(2,1)} custom-call(f32[512,896]{1,0:T(8,128)} %shard_map.49.refs_0_, f32[1,7168]{1,0:T(1,128)} %reshape.27.refs_1_, bf16[512,512]{1,0:T(8,128)(2,1)} %copy-done.9, bf16[512,384]{1,0:T(8,128)(2,1)} %copy-done.11), custom_call_target="tpu_custom_call" | custom-call | tf_op jit(solution)/shard_map/pallas_call | solution.py:234
  (65 shorter events, 0.2 us)
Async XLA Ops:
  1.4 8.3 %copy-start.21 = (f32[224]{0:T(256)S(1)}, f32[224]{0:T(256)}, u32[]{:S(2)}) copy-start(f32[224]{0:T(256)} %param.7) | copy-start | bytes 2692
  5.0 10.1 %collective-permute-start.7 = (bf16[160,896]{1,0:T(8,128)(2,1)}, bf16[160,896]{1,0:T(8,128)(2,1)S(1)}, u32[]{:S(2)}, u32[]{:S(2)}) collective-permute-start(bf16[160,896]{1,0:T(8,128)(2,1)} %get-tuple-element.22), channel_id=1, source_target_pairs={{0,1},{1,0},{2,3},{3,2},{4,5},{5,4},{6,7},{7,6},{8,9},{9,8},{10,11... | collective-permute-start | bytes 860168 | tf_op jit(solution)/shard_map/ppermute | solution.py:27
  8.1 9.9 %collective-permute-start.8 = (bf16[160,896]{1,0:T(8,128)(2,1)}, bf16[160,896]{1,0:T(8,128)(2,1)S(1)}, u32[]{:S(2)}, u32[]{:S(2)}) collective-permute-start(bf16[160,896]{1,0:T(8,128)(2,1)} %get-tuple-element.23), channel_id=1, source_target_pairs={{0,2},{1,3},{2,0},{3,1},{4,6},{5,7},{6,4},{7,5},{8,10},{9,11},{10,... | collective-permute-start | bytes 860168 | tf_op jit(solution)/shard_map/ppermute | solution.py:27
  9.7 12.9 %collective-permute-start.9 = (bf16[160,896]{1,0:T(8,128)(2,1)}, bf16[160,896]{1,0:T(8,128)(2,1)S(1)}, u32[]{:S(2)}, u32[]{:S(2)}) collective-permute-start(bf16[160,896]{1,0:T(8,128)(2,1)} %get-tuple-element.24), channel_id=1, source_target_pairs={{0,3},{1,2},{2,1},{3,0},{4,7},{5,6},{6,5},{7,4},{8,11},{9,10},{10,... | collective-permute-start | bytes 860168 | tf_op jit(solution)/shard_map/ppermute | solution.py:27
  9.7 17.6 %collective-permute-start.13 = (f32[1,224]{1,0:T(1,128)S(1)}, f32[1,224]{1,0:T(1,128)S(1)}, u32[]{:S(2)}, u32[]{:S(2)}) collective-permute-start(f32[1,224]{1,0:T(1,128)S(1)} %bitcast.4), channel_id=1, source_target_pairs={{0,1},{1,0},{2,3},{3,2},{4,5},{5,4},{6,7},{7,6},{8,9},{9,8},{10,11... | collective-permute-start | bytes 2696 | tf_op jit(solution)/shard_map/ppermute | solution.py:27
  15.2 7.4 %copy-start.12 = (bf16[160,896]{1,0:T(8,128)(2,1)}, bf16[160,896]{1,0:T(8,128)(2,1)S(1)}, u32[]{:S(2)}) copy-start(bf16[160,896]{1,0:T(8,128)(2,1)S(1)} %collective-permute-done.7.refs_1_) | copy-start | bytes 860164
  18.0 4.5 %copy-start.13 = (bf16[160,896]{1,0:T(8,128)(2,1)}, bf16[160,896]{1,0:T(8,128)(2,1)S(1)}, u32[]{:S(2)}) copy-start(bf16[160,896]{1,0:T(8,128)(2,1)S(1)} %collective-permute-done.8.refs_2_) | copy-start | bytes 860164
  22.5 0.7 copy-start.14
  25.6 53.7 %collective-permute-start.11 = (bf16[640,896]{1,0:T(8,128)(2,1)}, bf16[640,896]{1,0:T(8,128)(2,1)}, u32[]{:S(2)}, u32[]{:S(2)}) collective-permute-start(bf16[640,896]{1,0:T(8,128)(2,1)} %shard_map.48.refs_8_), channel_id=1, source_target_pairs={{0,16},{8,24},{16,0},{24,8},{1,17},{9,25},{17,1},{25,9},{2,18},{10... | collective-permute-start | bytes 3440648 | tf_op jit(solution)/shard_map/ppermute | solution.py:27
  27.3 8.8 %collective-permute-start.14 = (f32[2,224]{1,0:T(2,128)S(1)}, f32[2,224]{1,0:T(2,128)S(1)}, u32[]{:S(2)}, u32[]{:S(2)}) collective-permute-start(f32[2,224]{1,0:T(2,128)S(1)} %pad_maximum_fusion.2), channel_id=1, source_target_pairs={{0,2},{1,3},{2,0},{3,1},{4,6},{5,7},{6,4},{7,5},{8,10},{9,11},{10,... | collective-permute-start | bytes 5384 | tf_op jit(solution)/shard_map/ppermute | solution.py:27
  32.5 11.8 %collective-permute-start.25 = (bf16[160,384]{1,0:T(8,128)(2,1)}, bf16[160,384]{1,0:T(8,128)(2,1)S(1)}, u32[]{:S(2)}, u32[]{:S(2)}) collective-permute-start(bf16[160,384]{1,0:T(8,128)(2,1)} %get-tuple-element.30), channel_id=1, source_target_pairs={{0,1},{1,0},{2,3},{3,2},{4,5},{5,4},{6,7},{7,6},{8,9},{9,8},{10,11... | collective-permute-start | bytes 368648 | tf_op jit(solution)/shard_map/ppermute | solution.py:27
  34.1 11.8 %collective-permute-start.26 = (bf16[160,384]{1,0:T(8,128)(2,1)}, bf16[160,384]{1,0:T(8,128)(2,1)S(1)}, u32[]{:S(2)}, u32[]{:S(2)}) collective-permute-start(bf16[160,384]{1,0:T(8,128)(2,1)} %get-tuple-element.31), channel_id=1, source_target_pairs={{0,2},{1,3},{2,0},{3,1},{4,6},{5,7},{6,4},{7,5},{8,10},{9,11},{10,... | collective-permute-start | bytes 368648 | tf_op jit(solution)/shard_map/ppermute | solution.py:27
  34.6 11.9 %collective-permute-start.27 = (bf16[160,384]{1,0:T(8,128)(2,1)}, bf16[160,384]{1,0:T(8,128)(2,1)S(1)}, u32[]{:S(2)}, u32[]{:S(2)}) collective-permute-start(bf16[160,384]{1,0:T(8,128)(2,1)} %get-tuple-element.32), channel_id=1, source_target_pairs={{0,3},{1,2},{2,1},{3,0},{4,7},{5,6},{6,5},{7,4},{8,11},{9,10},{10,... | collective-permute-start | bytes 368648 | tf_op jit(solution)/shard_map/ppermute | solution.py:27
  36.1 4.6 %collective-permute-start.15 = (f32[4,224]{1,0:T(4,128)S(1)}, f32[4,224]{1,0:T(4,128)S(1)}, u32[]{:S(2)}, u32[]{:S(2)}) collective-permute-start(f32[4,224]{1,0:T(4,128)S(1)} %pad_maximum_fusion.1), channel_id=1, source_target_pairs={{0,4},{1,5},{2,6},{3,7},{4,0},{5,1},{6,2},{7,3},{8,12},{9,13},{10,... | collective-permute-start | bytes 10760 | tf_op jit(solution)/shard_map/ppermute | solution.py:27
  40.7 6.8 %collective-permute-start.18 = (bf16[160,512]{1,0:T(8,128)(2,1)}, bf16[160,512]{1,0:T(8,128)(2,1)S(1)}, u32[]{:S(2)}, u32[]{:S(2)}) collective-permute-start(bf16[160,512]{1,0:T(8,128)(2,1)} %get-tuple-element.26), channel_id=1, source_target_pairs={{0,1},{1,0},{2,3},{3,2},{4,5},{5,4},{6,7},{7,6},{8,9},{9,8},{10,11... | collective-permute-start | bytes 491528 | tf_op jit(solution)/shard_map/ppermute | solution.py:27
  44.4 5.5 %copy-start.18 = (bf16[160,384]{1,0:T(8,128)(2,1)}, bf16[160,384]{1,0:T(8,128)(2,1)S(1)}, u32[]{:S(2)}) copy-start(bf16[160,384]{1,0:T(8,128)(2,1)S(1)} %collective-permute-done.25.refs_1_) | copy-start | bytes 368644
  44.4 7.6 %collective-permute-start.19 = (bf16[160,512]{1,0:T(8,128)(2,1)}, bf16[160,512]{1,0:T(8,128)(2,1)S(1)}, u32[]{:S(2)}, u32[]{:S(2)}) collective-permute-start(bf16[160,512]{1,0:T(8,128)(2,1)} %get-tuple-element.27), channel_id=1, source_target_pairs={{0,2},{1,3},{2,0},{3,1},{4,6},{5,7},{6,4},{7,5},{8,10},{9,11},{10,... | collective-permute-start | bytes 491528 | tf_op jit(solution)/shard_map/ppermute | solution.py:27
  45.9 4.0 %copy-start.19 = (bf16[160,384]{1,0:T(8,128)(2,1)}, bf16[160,384]{1,0:T(8,128)(2,1)S(1)}, u32[]{:S(2)}) copy-start(bf16[160,384]{1,0:T(8,128)(2,1)S(1)} %collective-permute-done.26.refs_2_) | copy-start | bytes 368644
  46.0 14.6 %collective-permute-start.1 = (bf16[64,2560]{1,0:T(8,128)(2,1)}, bf16[64,2560]{1,0:T(8,128)(2,1)S(1)}, u32[]{:S(2)}, u32[]{:S(2)}) collective-permute-start(bf16[64,2560]{1,0:T(8,128)(2,1)} %get-tuple-element.19.refs_0_), channel_id=1, source_target_pairs={{0,2},{1,3},{2,0},{3,1},{4,6},{5,7},{6,4},{7,5},{8,10},{9,11},{10,... | collective-permute-start | bytes 983048 | tf_op jit(solution)/shard_map/ppermute | solution.py:27
  46.4 3.5 %copy-start.20 = (bf16[160,384]{1,0:T(8,128)(2,1)}, bf16[160,384]{1,0:T(8,128)(2,1)S(1)}, u32[]{:S(2)}) copy-start(bf16[160,384]{1,0:T(8,128)(2,1)S(1)} %collective-permute-done.27.refs_3_) | copy-start | bytes 368644
  46.4 17.6 %collective-permute-start = (bf16[64,2560]{1,0:T(8,128)(2,1)}, bf16[64,2560]{1,0:T(8,128)(2,1)S(1)}, u32[]{:S(2)}, u32[]{:S(2)}) collective-permute-start(bf16[64,2560]{1,0:T(8,128)(2,1)} %get-tuple-element.19.refs_0_), channel_id=1, source_target_pairs={{0,1},{1,0},{2,3},{3,2},{4,5},{5,4},{6,7},{7,6},{8,9},{9,8},{10,11... | collective-permute-start | bytes 983048 | tf_op jit(solution)/shard_map/ppermute | solution.py:27
  47.5 14.5 %copy-start.15 = (bf16[160,512]{1,0:T(8,128)(2,1)}, bf16[160,512]{1,0:T(8,128)(2,1)S(1)}, u32[]{:S(2)}) copy-start(bf16[160,512]{1,0:T(8,128)(2,1)S(1)} %collective-permute-done.18.refs_1_) | copy-start | bytes 491524
  47.5 13.0 %collective-permute-start.20 = (bf16[160,512]{1,0:T(8,128)(2,1)}, bf16[160,512]{1,0:T(8,128)(2,1)S(1)}, u32[]{:S(2)}, u32[]{:S(2)}) collective-permute-start(bf16[160,512]{1,0:T(8,128)(2,1)} %get-tuple-element.28), channel_id=1, source_target_pairs={{0,3},{1,2},{2,1},{3,0},{4,7},{5,6},{6,5},{7,4},{8,11},{9,10},{10,... | collective-permute-start | bytes 491528 | tf_op jit(solution)/shard_map/ppermute | solution.py:27
  49.9 29.4 %copy-start = (bf16[640,896]{1,0:T(8,128)(2,1)S(1)}, bf16[640,896]{1,0:T(8,128)(2,1)}, u32[]{:S(2)}) copy-start(bf16[640,896]{1,0:T(8,128)(2,1)} %shard_map.48.refs_8_) | copy-start | bytes 3440644
  51.9 10.0 %copy-start.16 = (bf16[160,512]{1,0:T(8,128)(2,1)}, bf16[160,512]{1,0:T(8,128)(2,1)S(1)}, u32[]{:S(2)}) copy-start(bf16[160,512]{1,0:T(8,128)(2,1)S(1)} %collective-permute-done.19.refs_2_) | copy-start | bytes 491524
  51.9 20.3 %collective-permute-start.29 = (bf16[640,384]{1,0:T(8,128)(2,1)}, bf16[640,384]{1,0:T(8,128)(2,1)S(1)}, u32[]{:S(2)}, u32[]{:S(2)}) collective-permute-start(bf16[640,384]{1,0:T(8,128)(2,1)} %shard_map.53.refs_8_), channel_id=1, source_target_pairs={{0,16},{8,24},{16,0},{24,8},{1,17},{9,25},{17,1},{25,9},{2,18},{10... | collective-permute-start | bytes 1474568 | tf_op jit(solution)/shard_map/ppermute | solution.py:27
  60.5 1.5 %copy-start.17 = (bf16[160,512]{1,0:T(8,128)(2,1)}, bf16[160,512]{1,0:T(8,128)(2,1)S(1)}, u32[]{:S(2)}) copy-start(bf16[160,512]{1,0:T(8,128)(2,1)S(1)} %collective-permute-done.20.refs_3_) | copy-start | bytes 491524
  60.5 11.7 %collective-permute-start.3 = (bf16[64,2560]{1,0:T(8,128)(2,1)}, bf16[64,2560]{1,0:T(8,128)(2,1)S(1)}, u32[]{:S(2)}, u32[]{:S(2)}) collective-permute-start(bf16[64,2560]{1,0:T(8,128)(2,1)} %get-tuple-element.20), channel_id=1, source_target_pairs={{0,4},{1,5},{2,6},{3,7},{4,0},{5,1},{6,2},{7,3},{8,12},{9,13},{10,... | collective-permute-start | bytes 983048 | tf_op jit(solution)/shard_map/ppermute | solution.py:27
  60.5 31.3 %copy-start.1 = (bf16[64,2560]{1,0:T(8,128)(2,1)}, bf16[64,2560]{1,0:T(8,128)(2,1)S(1)}, u32[]{:S(2)}) copy-start(bf16[64,2560]{1,0:T(8,128)(2,1)S(1)} %collective-permute-done.1.refs_2_) | copy-start | bytes 983044
  60.5 12.6 %collective-permute-start.2 = (bf16[64,2560]{1,0:T(8,128)(2,1)S(1)}, bf16[64,2560]{1,0:T(8,128)(2,1)S(1)}, u32[]{:S(2)}, u32[]{:S(2)}) collective-permute-start(bf16[64,2560]{1,0:T(8,128)(2,1)S(1)} %collective-permute-done.1.refs_2_), channel_id=1, source_target_pairs={{0,1},{1,0},{2,3},{3,2},{4,5},{5,4},{6,7},{7,6},{8,9},{9,8},{10,11... | collective-permute-start | bytes 983048 | tf_op jit(solution)/shard_map/ppermute | solution.py:27
  64.0 27.8 %copy-start.2 = (bf16[64,2560]{1,0:T(8,128)(2,1)}, bf16[64,2560]{1,0:T(8,128)(2,1)S(1)}, u32[]{:S(2)}) copy-start(bf16[64,2560]{1,0:T(8,128)(2,1)S(1)} %collective-permute-done.refs_1_) | copy-start | bytes 983044
  64.0 20.4 %collective-permute-start.22 = (bf16[640,512]{1,0:T(8,128)(2,1)}, bf16[640,512]{1,0:T(8,128)(2,1)}, u32[]{:S(2)}, u32[]{:S(2)}) collective-permute-start(bf16[640,512]{1,0:T(8,128)(2,1)} %shard_map.51.refs_8_), channel_id=1, source_target_pairs={{0,16},{8,24},{16,0},{24,8},{1,17},{9,25},{17,1},{25,9},{2,18},{10... | collective-permute-start | bytes 1966088 | tf_op jit(solution)/shard_map/ppermute | solution.py:27
  72.2 19.6 %copy-start.3 = (bf16[64,2560]{1,0:T(8,128)(2,1)}, bf16[64,2560]{1,0:T(8,128)(2,1)S(1)}, u32[]{:S(2)}) copy-start(bf16[64,2560]{1,0:T(8,128)(2,1)S(1)} %collective-permute-done.3.refs_4_) | copy-start | bytes 983044
  72.2 7.1 %collective-permute-start.4 = (bf16[64,2560]{1,0:T(8,128)(2,1)S(1)}, bf16[64,2560]{1,0:T(8,128)(2,1)S(1)}, u32[]{:S(2)}, u32[]{:S(2)}) collective-permute-start(bf16[64,2560]{1,0:T(8,128)(2,1)S(1)} %collective-permute-done.3.refs_4_), channel_id=1, source_target_pairs={{0,1},{1,0},{2,3},{3,2},{4,5},{5,4},{6,7},{7,6},{8,9},{9,8},{10,11... | collective-permute-start | bytes 983048 | tf_op jit(solution)/shard_map/ppermute | solution.py:27
  72.2 0.9 copy-start.10
  72.2 12.2 %collective-permute-start.21 = (bf16[640,512]{1,0:T(8,128)(2,1)}, bf16[640,512]{1,0:T(8,128)(2,1)S(1)}, u32[]{:S(2)}, u32[]{:S(2)}) collective-permute-start(bf16[640,512]{1,0:T(8,128)(2,1)} %shard_map.51.refs_8_), channel_id=1, source_target_pairs={{0,8},{8,0},{16,24},{24,16},{1,9},{9,1},{17,25},{25,17},{2,10},{10... | collective-permute-start | bytes 1966088 | tf_op jit(solution)/shard_map/ppermute | solution.py:27
  73.1 18.7 %copy-start.4 = (bf16[64,2560]{1,0:T(8,128)(2,1)}, bf16[64,2560]{1,0:T(8,128)(2,1)S(1)}, u32[]{:S(2)}) copy-start(bf16[64,2560]{1,0:T(8,128)(2,1)S(1)} %collective-permute-done.2.refs_3_) | copy-start | bytes 983044
  73.1 9.4 %collective-permute-start.5 = (bf16[64,2560]{1,0:T(8,128)(2,1)S(1)}, bf16[64,2560]{1,0:T(8,128)(2,1)S(1)}, u32[]{:S(2)}, u32[]{:S(2)}) collective-permute-start(bf16[64,2560]{1,0:T(8,128)(2,1)S(1)} %collective-permute-done.3.refs_4_), channel_id=1, source_target_pairs={{0,2},{1,3},{2,0},{3,1},{4,6},{5,7},{6,4},{7,5},{8,10},{9,11},{10,... | collective-permute-start | bytes 983048 | tf_op jit(solution)/shard_map/ppermute | solution.py:27
  79.3 12.5 %copy-start.5 = (bf16[64,2560]{1,0:T(8,128)(2,1)}, bf16[64,2560]{1,0:T(8,128)(2,1)S(1)}, u32[]{:S(2)}) copy-start(bf16[64,2560]{1,0:T(8,128)(2,1)S(1)} %collective-permute-done.4.refs_5_) | copy-start | bytes 983044
  79.3 31.7 %collective-permute-start.10 = (bf16[640,896]{1,0:T(8,128)(2,1)S(1)}, bf16[640,896]{1,0:T(8,128)(2,1)}, u32[]{:S(2)}, u32[]{:S(2)}) collective-permute-start(bf16[640,896]{1,0:T(8,128)(2,1)S(1)} %copy-done), channel_id=1, source_target_pairs={{0,8},{8,0},{16,24},{24,16},{1,9},{9,1},{17,25},{25,17},{2,10},{10... | collective-permute-start | bytes 3440648 | tf_op jit(solution)/shard_map/ppermute | solution.py:27
  79.3 31.7 %collective-permute-start.12 = (bf16[640,896]{1,0:T(8,128)(2,1)}, bf16[640,896]{1,0:T(8,128)(2,1)}, u32[]{:S(2)}, u32[]{:S(2)}) collective-permute-start(bf16[640,896]{1,0:T(8,128)(2,1)} %collective-permute-done.11.refs_10_), channel_id=1, source_target_pairs={{0,8},{8,0},{16,24},{24,16},{1,9},{9,1},{17,25},{25,17},{2,10},{10... | collective-permute-start | bytes 3440648 | tf_op jit(solution)/shard_map/ppermute | solution.py:27
  82.5 9.4 %copy-start.6 = (bf16[64,2560]{1,0:T(8,128)(2,1)}, bf16[64,2560]{1,0:T(8,128)(2,1)S(1)}, u32[]{:S(2)}) copy-start(bf16[64,2560]{1,0:T(8,128)(2,1)S(1)} %collective-permute-done.5.refs_6_) | copy-start | bytes 983044
  82.5 8.7 %collective-permute-start.6 = (bf16[64,2560]{1,0:T(8,128)(2,1)S(1)}, bf16[64,2560]{1,0:T(8,128)(2,1)S(1)}, u32[]{:S(2)}, u32[]{:S(2)}) collective-permute-start(bf16[64,2560]{1,0:T(8,128)(2,1)S(1)} %collective-permute-done.5.refs_6_), channel_id=1, source_target_pairs={{0,1},{1,0},{2,3},{3,2},{4,5},{5,4},{6,7},{7,6},{8,9},{9,8},{10,11... | collective-permute-start | bytes 983048 | tf_op jit(solution)/shard_map/ppermute | solution.py:27
  84.4 6.8 %collective-permute-start.23 = (bf16[640,512]{1,0:T(8,128)(2,1)}, bf16[640,512]{1,0:T(8,128)(2,1)}, u32[]{:S(2)}, u32[]{:S(2)}) collective-permute-start(bf16[640,512]{1,0:T(8,128)(2,1)} %collective-permute-done.22.refs_10_), channel_id=1, source_target_pairs={{0,8},{8,0},{16,24},{24,16},{1,9},{9,1},{17,25},{25,17},{2,10},{10... | collective-permute-start | bytes 1966088 | tf_op jit(solution)/shard_map/ppermute | solution.py:27
  84.5 6.8 %copy-start.8 = (bf16[640,512]{1,0:T(8,128)(2,1)}, bf16[640,512]{1,0:T(8,128)(2,1)S(1)}, u32[]{:S(2)}) copy-start(bf16[640,512]{1,0:T(8,128)(2,1)S(1)} %collective-permute-done.21.refs_9_) | copy-start | bytes 1966084
  84.5 12.6 %collective-permute-start.28 = (bf16[640,384]{1,0:T(8,128)(2,1)}, bf16[640,384]{1,0:T(8,128)(2,1)}, u32[]{:S(2)}, u32[]{:S(2)}) collective-permute-start(bf16[640,384]{1,0:T(8,128)(2,1)} %shard_map.53.refs_8_), channel_id=1, source_target_pairs={{0,8},{8,0},{16,24},{24,16},{1,9},{9,1},{17,25},{25,17},{2,10},{10... | collective-permute-start | bytes 1474568 | tf_op jit(solution)/shard_map/ppermute | solution.py:27
  91.2 0.7 copy-start.7
  91.2 5.9 %collective-permute-start.30 = (bf16[640,384]{1,0:T(8,128)(2,1)}, bf16[640,384]{1,0:T(8,128)(2,1)}, u32[]{:S(2)}, u32[]{:S(2)}) collective-permute-start(bf16[640,384]{1,0:T(8,128)(2,1)} %copy-done.10), channel_id=1, source_target_pairs={{0,8},{8,0},{16,24},{24,16},{1,9},{9,1},{17,25},{25,17},{2,10},{10... | collective-permute-start | bytes 1474568 | tf_op jit(solution)/shard_map/ppermute | solution.py:27
  91.3 14.6 %collective-permute-start.16 = (f32[8,224]{1,0:T(8,128)S(1)}, f32[8,224]{1,0:T(8,128)S(1)}, u32[]{:S(2)}, u32[]{:S(2)}) collective-permute-start(f32[8,224]{1,0:T(8,128)S(1)} %pad_maximum_fusion), channel_id=1, source_target_pairs={{0,8},{8,0},{16,24},{24,16},{1,9},{9,1},{17,25},{25,17},{2,10},{10... | collective-permute-start | bytes 21512 | tf_op jit(solution)/shard_map/ppermute | solution.py:27
  97.1 43.1 %collective-permute-start.24 = (bf16[512,512]{1,0:T(8,128)(2,1)}, bf16[512,512]{1,0:T(8,128)(2,1)S(1)}, u32[]{:S(2)}, u32[]{:S(2)}) collective-permute-start(bf16[512,512]{1,0:T(8,128)(2,1)} %shard_map.52), channel_id=1, source_target_pairs={{0,4},{1,5},{2,6},{3,7},{4,0},{5,1},{6,2},{7,3},{8,12},{9,13},{10,... | collective-permute-start | bytes 1572872 | tf_op jit(solution)/shard_map/ppermute | solution.py:27
  103.0 37.2 %collective-permute-start.31 = (bf16[512,384]{1,0:T(8,128)(2,1)}, bf16[512,384]{1,0:T(8,128)(2,1)S(1)}, u32[]{:S(2)}, u32[]{:S(2)}) collective-permute-start(bf16[512,384]{1,0:T(8,128)(2,1)} %shard_map.54), channel_id=1, source_target_pairs={{0,4},{1,5},{2,6},{3,7},{4,0},{5,1},{6,2},{7,3},{8,12},{9,13},{10,... | collective-permute-start | bytes 1179656 | tf_op jit(solution)/shard_map/ppermute | solution.py:27
  105.9 3.8 %collective-permute-start.17 = (f32[16,224]{1,0:T(8,128)S(1)}, f32[16,224]{1,0:T(8,128)S(1)}, u32[]{:S(2)}, u32[]{:S(2)}) collective-permute-start(f32[16,224]{1,0:T(8,128)S(1)} %concatenate.22), channel_id=1, source_target_pairs={{0,16},{8,24},{16,0},{24,8},{1,17},{9,25},{17,1},{25,9},{2,18},{10... | collective-permute-start | bytes 43016 | tf_op jit(solution)/shard_map/ppermute | solution.py:27
  140.1 0.8 copy-start.11
  140.9 0.8 copy-start.9
